TPU v7x, 32 devices: a whole 2x2x4 slice. The times are simulated.
32 devices in a mesh: aa: 4 (over y, x), ba: 2 (over core), col: 4 (over z).
Axes of the slice: x: 2, y: 2, z: 4, core: 2. Of those that a mesh axis runs over, the one named last changes fastest.
Arguments:
- tokens: bfloat16 [1024, 7168], P('aa', ('ba', 'col')), may hold values from -6 to 6
- expert_ids: int32 [1024, 8], P('aa'), may hold values from 0 to 383, as said below
- route_weight: float32 [1024, 8], P('aa'), may hold values from 0.5 to 2
- w_gate: bfloat16 [4, 7168, 2048], P('aa', None, ('ba', 'col')), may hold values from -0.0625 to 0.0625
- w_up: bfloat16 [4, 7168, 2048], P('aa', None, ('ba', 'col')), may hold values from -0.0625 to 0.0625
- w_down: bfloat16 [4, 2048, 7168], P('aa', ('ba', 'col')), may hold values from -0.125 to 0.125
Outputs:
- mixed: bfloat16 [1024, 7168], P('aa', ('ba', 'col'))
Inputs may be any that keep to these rules, and one draw needn't show every extreme that they name: `expert_ids`: each row names 8 different experts.
All inputs are finite; a program needn't handle non-finite values.
Results may differ from a plain program's by a relative error of at most 0.015.
Values may be sent and summed in bfloat16 or wider, within the bound.
A program may use at most 64 MiB of HBM per device.

v0:
```python
import jax
import jax.numpy as jnp
from jax import lax
from jax.sharding import PartitionSpec as P

CAP = 8


def routing(expert_ids, route_weight, flight, capacity):
    expert_pool = jnp.arange(flight, dtype=jnp.int32)
    matched = expert_ids[:, :, None] == expert_pool[None, None, :]
    counted = jnp.sum(matched.astype(jnp.int32), axis=1)
    shares = jnp.sum(jnp.where(matched, route_weight[:, :, None], 0.0), axis=1)
    before = jnp.cumsum(counted, axis=0) - counted
    retained = (counted > 0) & (before < capacity)
    placed = retained[:, :, None] & (
        before[:, :, None] == jnp.arange(capacity, dtype=jnp.int32)[None, None, :]
    )
    return (placed, shares)


def shards(tokens, expert_ids, route_weight, w_gate, w_up, w_down):
    flight = lax.axis_size("aa")
    placed, shares = routing(expert_ids, route_weight, flight, CAP)
    chooser = placed.astype(jnp.bfloat16)
    local_slice = jnp.einsum(
        "tec,tf->ecf", chooser, tokens, preferred_element_type=jnp.float32
    ).astype(jnp.bfloat16)
    gate_matrix = w_gate[0]
    up_matrix = w_up[0]
    down_matrix = w_down[0]
    arrived = lax.all_to_all(local_slice, "aa", split_axis=0, concat_axis=0, tiled=True)
    flat_rows = arrived.reshape(-1, arrived.shape[2])
    portion = lax.all_gather(flat_rows, ("ba", "col"), axis=1, tiled=True)
    gate_sum = jnp.dot(portion, gate_matrix, preferred_element_type=jnp.float32)
    up_sum = jnp.dot(portion, up_matrix, preferred_element_type=jnp.float32)
    hidden = (jax.nn.silu(gate_sum) * up_sum).astype(jnp.bfloat16)
    partial_value = jnp.dot(hidden, down_matrix, preferred_element_type=jnp.float32).astype(
        jnp.bfloat16
    )
    shaped = partial_value.reshape(flight, CAP, partial_value.shape[1])
    returned = lax.all_to_all(shaped, "aa", split_axis=0, concat_axis=0, tiled=True)
    merged = lax.psum_scatter(
        returned.astype(jnp.float32).astype(jnp.bfloat16),
        ("ba", "col"),
        scatter_dimension=2,
        tiled=True,
    )
    combine_weight = placed.astype(jnp.float32) * shares[:, :, None]
    weight_high = combine_weight.astype(jnp.bfloat16)
    weight_low = (combine_weight - weight_high.astype(jnp.float32)).astype(jnp.bfloat16)
    mixed = jnp.einsum("tec,ecf->tf", weight_high, merged, preferred_element_type=jnp.float32)
    mixed = mixed + jnp.einsum(
        "tec,ecf->tf", weight_low, merged, preferred_element_type=jnp.float32
    )
    return mixed.astype(jnp.bfloat16)


def solution(mesh):
    in_specs = (
        P("aa", ("ba", "col")),
        P("aa", None),
        P("aa", None),
        P("aa", None, ("ba", "col")),
        P("aa", None, ("ba", "col")),
        P("aa", ("ba", "col"), None),
    )
    out_specs = P("aa", ("ba", "col"))
    return jax.shard_map(shards, mesh=mesh, in_specs=in_specs, out_specs=out_specs, check_vma=False)
```

profile of v0, /device:TPU:0, one launch (start us, length us, event | category | flops | bytes accessed | tf_op | source)
XLA Modules:
  0.0 133.6 jit_solution(12846665382784906666)
XLA Ops:
  6.5 0.0 copy-start
  6.5 0.0 reduce-scatter.4.cloned.1.call-start
  6.5 0.8 convert_reduce_fusion
  7.3 1.2 reduce-window.6
  8.5 0.1 slice.8
  8.6 0.1 copy.15
  8.8 0.1 copy.16
  8.9 0.1 add_bitcast_fusion
  9.0 0.0 copy-done
  9.0 0.2 convolution_convert_fusion.1
  9.1 9.8 %all_to_all.10 = bf16[4,8,896]{2,1,0:T(8,128)(2,1)S(1)} all-to-all(bf16[4,8,896]{2,1,0:T(8,128)(2,1)S(1)} %convolution_convert_fusion.1), channel_id=1, replica_groups=mesh['aa'=4,'ba'=2,'col'=4] {'aa'}, dimensions={0} | all-to-all | bytes 114688 | tf_op jit(solution)/shard_map/all_to_all | solution.py:32
  19.0 26.4 %all_gather.3 = bf16[32,7168]{1,0:T(8,128)(2,1)S(1)} all-gather(bf16[32,896]{1,0:T(8,128)(2,1)S(1)} %bitcast.51), channel_id=1, replica_groups=mesh['aa'=4,'ba'=2,'col'=4] {'ba','col'}, dimensions={1}, use_global_device_ids=true | all-gather | bytes 516096 | tf_op jit(solution)/shard_map/all_gather | solution.py:34
  45.3 2.8 %fusion.4 = f32[32,256]{1,0:T(8,128)S(1)} fusion(bf16[32,7168]{1,0:T(8,128)(2,1)S(1)} %all_gather.3, bf16[1,7168,256]{2,1,0:T(8,128)(2,1)} %param.9), kind=kOutput, calls=%fused_computation.5 | convolution fusion | flops 117440512 | bytes 4161536 | tf_op jit(solution)/shard_map/dot_general | solution.py:35
  48.1 5.2 %fusion = bf16[4,8,7168]{2,1,0:T(8,128)(2,1)S(1)} fusion(bf16[1,256,7168]{2,1,0:T(8,128)(2,1)} %param.11, bf16[32,7168]{1,0:T(8,128)(2,1)S(1)} %all_gather.3, bf16[1,7168,256]{2,1,0:T(8,128)(2,1)} %param.10, f32[32,256]{1,0:T(8,128)S(1)} %fusion.4), kind=kOutput, calls=%fused_computation.1 | convolution fusion | flops 235159552 | bytes 8290304 | tf_op jit(solution)/shard_map/dot_general | solution.py:38
  53.3 11.2 %all_to_all.11 = bf16[4,8,7168]{2,1,0:T(8,128)(2,1)S(1)} all-to-all(bf16[4,8,7168]{2,1,0:T(8,128)(2,1)S(1)} %fusion), channel_id=1, replica_groups=mesh['aa'=4,'ba'=2,'col'=4] {'aa'}, dimensions={0} | all-to-all | bytes 917504 | tf_op jit(solution)/shard_map/all_to_all | solution.py:42
  64.6 7.2 %copy.17 = bf16[4,8,7168]{1,0,2:T(4,128)(2,1)} copy(bf16[4,8,7168]{2,1,0:T(8,128)(2,1)S(1)} %all_to_all.11) | data formatting | bytes 917504
  71.7 0.0 copy-start.1
  71.7 0.0 copy-start.2
  71.7 9.6 %reshape.28 = bf16[7168,32]{1,0:T(8,128)(2,1)} reshape(bf16[7168,4,8]{2,1,0:T(4,128)(2,1)} %bitcast.49) | data formatting | bytes 917504
  81.3 0.0 reduce-scatter.4.cloned.1.call-update
  81.3 0.0 copy-done.1
  81.3 0.0 copy-done.2
  81.4 41.1 %reduce-scatter.4.cloned.1.call-done = bf16[896,32]{1,0:T(8,128)(2,1)} async-done(((bf16[7168,32]{1,0:T(8,128)(2,1)}), bf16[896,32]{1,0:T(8,128)(2,1)}) %reduce-scatter.4.cloned.1.call-update) | async-done | bytes 57360
  122.5 1.9 %reshape.29 = bf16[896,4,8]{2,1,0:T(4,128)(2,1)S(1)} reshape(bf16[896,32]{1,0:T(8,128)(2,1)} %reduce-scatter.4.cloned.1.call-done) | data formatting | bytes 114688
  124.4 0.9 copy.18
  125.3 0.3 convolution_bitcast_fusion
  125.7 1.1 fusion.7
  (5 shorter events, 0.1 us)
Async XLA Ops:
  6.5 2.4 %copy-start = (bf16[256,896]{1,0:T(8,128)(2,1)S(1)}, bf16[256,896]{1,0:T(8,128)(2,1)}, u32[]{:S(2)}) copy-start(bf16[256,896]{1,0:T(8,128)(2,1)} %param.6) | copy-start | bytes 1376260
  6.5 115.9 %reduce-scatter.4.cloned.1.call-start = ((), (), s32[]{:S(2)}) async-start(), calls=%async_computation.3 | async-start | bytes 2064384
  71.7 9.6 %copy-start.1 = (s32[256,8]{0,1:T(8,128)S(1)}, s32[256,8]{0,1:T(8,128)}, u32[]{:S(2)}) copy-start(s32[256,8]{0,1:T(8,128)} %param.7) | copy-start | bytes 24580
  71.7 9.6 %copy-start.2 = (f32[256,8]{0,1:T(8,128)S(1)}, f32[256,8]{0,1:T(8,128)}, u32[]{:S(2)}) copy-start(f32[256,8]{0,1:T(8,128)} %param.8) | copy-start | bytes 24580
Sparse Core Ops, SparseCore 0:
  81.4 40.9 reduce-scatter.3
where the time goes:
time: 134 us
  blocking collectives  47.4 us (35%)
  waiting for transfers between devices  41.1 us (31%)
  local copies, waits for them, and re-layouts  19.9 us (15%)
  between operations  13.4 us (10%)
  matrix products  9.63 us (7%)
  other arithmetic  2.13 us (2%)
    unnamed x2, waiting for transfers between devices  41.1 us
    all_gather x1, blocking collectives, shards(): portion = lax.all_gather(flat_rows, ('ba', 'col'), axis=1, tiled=True)  26.4 us
    unnamed x10, local copies, waits for them, and re-layouts  19.6 us
    all_to_all x1, blocking collectives, shards(): lax.all_to_all(shaped, 'aa', split_axis=0, concat_axis=0, tiled=True)  11.2 us
    all_to_all x1, blocking collectives, shards(): lax.all_to_all(local_slice, 'aa', split_axis=0, concat_axis=0, tiled=True)  9.82 us
    dot_general x1, matrix products, shards(): jnp.dot(hidden, down_matrix, preferred_element_type=jnp.float32)  5.25 us
    dot_general x1, matrix products, shards(): gate_sum = jnp.dot(portion, gate_matrix, preferred_element_type=jnp.float32)  2.76 us
  transfers between devices with their start and end apart: 1, of which 1 were waited for; matrix products, arithmetic and copies ran while one was open for 0% of the time, Pallas kernels for 0%

commit v1 on v0

v1 whole, which is shorter than its diff:
```python
import functools

import jax
import jax.numpy as jnp
from jax import lax
from jax.experimental import pallas as pl
from jax.experimental.pallas import tpu as pltpu
from jax.sharding import PartitionSpec as P

CAP = 8
MESH = pl.DeviceIdType.MESH
F32 = jnp.float32
BF16 = jnp.bfloat16


def kernel(
    E, B, Z,
    ids_hbm, rw_hbm, tok_hbm, wg_hbm, wu_hbm, wd_hbm,
    merged_ref, wt_ref,
    ids, rw, tok, wg, wu, wd, disp, xr, acc_g, acc_u, part, pr, total, rr,
    in_sem, wg_sem, wu_sem, wd_sem,
    d_send, d_recv, f_send, f_recv, p_send, p_recv, r_send, r_recv,
):
    a = lax.axis_index("aa")
    c = lax.axis_index("ba")
    z = lax.axis_index("col")
    N = B * Z
    T = tok.shape[0]
    W = tok.shape[1]
    rows = E * CAP

    def far_first():
        order = []
        for k in sorted(range(Z), key=lambda k: -min(k, Z - k)):
            for i in range(E):
                if (k, i) != (0, 0):
                    order.append((k, i))
        return order

    def at(k, n, base):
        return lax.rem(base + k, n)

    ins = [
        pltpu.make_async_copy(ids_hbm, ids, in_sem.at[0]),
        pltpu.make_async_copy(rw_hbm, rw, in_sem.at[1]),
        pltpu.make_async_copy(tok_hbm, tok, in_sem.at[2]),
    ]
    for copy in ins:
        copy.start()

    barrier = pltpu.get_barrier_semaphore()
    for k, i in far_first():
        pl.semaphore_signal(
            barrier, inc=1, device_id=(at(i, E, a), c, at(k, Z, z)), device_id_type=MESH
        )
    for b in range(1, B):
        pl.semaphore_signal(barrier, inc=1, device_id=(a, at(b, B, c), z), device_id_type=MESH)

    chunks = [(at(b, B, c), at(k, Z, z)) for k in range(Z) for b in range(B)]
    w_copies = []
    for cc, zz in chunks:
        j = cc * Z + zz
        span = pl.ds(pl.multiple_of(j * W, 128), W)
        for src, dst, sem in ((wg_hbm, wg, wg_sem), (wu_hbm, wu, wu_sem)):
            pltpu.make_async_copy(src.at[0, span, :], dst.at[j], sem.at[j]).start()
    for cc, zz in chunks:
        j = cc * Z + zz
        span = pl.ds(pl.multiple_of(j * W, 128), W)
        pltpu.make_async_copy(wd_hbm.at[0, :, span], wd.at[j], wd_sem.at[j]).start()

    ins[0].wait()
    ins[1].wait()
    expert = lax.broadcasted_iota(jnp.int32, (E, T), 0)
    counted = jnp.zeros((E, T), F32)
    shares = jnp.zeros((E, T), F32)
    for k in range(ids.shape[0]):
        match = jnp.broadcast_to(ids[k : k + 1, :], (E, T)) == expert
        counted = counted + jnp.where(match, 1.0, 0.0)
        shares = shares + jnp.where(match, jnp.broadcast_to(rw[k : k + 1, :], (E, T)), 0.0)
    earlier = lax.broadcasted_iota(jnp.int32, (T, T), 0) < lax.broadcasted_iota(
        jnp.int32, (T, T), 1
    )
    before = jnp.dot(
        counted.astype(BF16), jnp.where(earlier, 1.0, 0.0).astype(BF16), preferred_element_type=F32
    )
    slot = lax.broadcasted_iota(jnp.int32, (CAP, T), 0).astype(F32)
    placed = []
    weights = []
    for e in range(E):
        hit = jnp.broadcast_to(counted[e : e + 1, :], (CAP, T)) > 0.0
        rank = jnp.broadcast_to(before[e : e + 1, :], (CAP, T))
        one = jnp.where(hit & (rank == slot), 1.0, 0.0)
        placed.append(one)
        weights.append(one * jnp.broadcast_to(shares[e : e + 1, :], (CAP, T)))
    chooser = jnp.concatenate(placed, axis=0).astype(BF16)

    ins[2].wait()
    picked = jnp.dot(chooser, tok[...], preferred_element_type=F32)
    for e in range(E):
        disp[e] = picked[e * CAP : (e + 1) * CAP, :].astype(BF16)
    mine = c * Z + z
    xr[mine, a] = disp[a]

    pl.semaphore_wait(barrier, E * Z - 1 + B - 1)

    sends = []
    for k, i in far_first():
        aa, zz = at(i, E, a), at(k, Z, z)
        copy = pltpu.make_async_remote_copy(
            src_ref=disp.at[aa], dst_ref=xr.at[mine, a],
            send_sem=d_send.at[zz, aa], recv_sem=d_recv.at[z, a],
            device_id=(aa, c, zz), device_id_type=MESH,
        )
        copy.start()
        sends.append(copy)

    weight = jnp.concatenate(weights, axis=0)
    high = weight.astype(BF16)
    low = (weight - high.astype(F32)).astype(BF16)
    wt_ref[...] = jnp.concatenate([high, low], axis=0)

    acc_g[...] = jnp.zeros_like(acc_g)
    acc_u[...] = jnp.zeros_like(acc_u)

    def feed(j):
        span = pl.ds(pl.multiple_of(j * W, 128), W)
        x = xr[j].astype(F32).reshape(rows, W).astype(BF16)
        pltpu.make_async_copy(wg_hbm.at[0, span, :], wg.at[j], wg_sem.at[j]).wait()
        pltpu.make_async_copy(wu_hbm.at[0, span, :], wu.at[j], wu_sem.at[j]).wait()
        acc_g[...] += jnp.dot(x, wg[j], preferred_element_type=F32)
        acc_u[...] += jnp.dot(x, wu[j], preferred_element_type=F32)

    def feed_forwarded(k):
        zz = at(k, Z, z)
        for b in range(1, B):
            j = at(B - b, B, c) * Z + zz
            pltpu.make_async_remote_copy(
                src_ref=xr.at[j], dst_ref=xr.at[j],
                send_sem=f_send.at[b - 1, zz], recv_sem=f_recv.at[b - 1, zz],
                device_id=(a, at(b, B, c), z), device_id_type=MESH,
            ).wait_recv()
            feed(j)

    for k in range(Z):
        zz = at(k, Z, z)
        j = c * Z + zz
        for i in range(E):
            if (k, i) != (0, 0):
                aa = at(i, E, a)
                pltpu.make_async_remote_copy(
                    src_ref=xr.at[j, aa], dst_ref=xr.at[j, aa],
                    send_sem=d_send.at[zz, aa], recv_sem=d_recv.at[zz, aa],
                    device_id=(a, at(1, B, c), z), device_id_type=MESH,
                ).wait_recv()
        for b in range(1, B):
            copy = pltpu.make_async_remote_copy(
                src_ref=xr.at[j], dst_ref=xr.at[j],
                send_sem=f_send.at[b - 1, zz], recv_sem=f_recv.at[b - 1, zz],
                device_id=(a, at(b, B, c), z), device_id_type=MESH,
            )
            copy.start()
            sends.append(copy)
        feed(j)
        if k > 0:
            feed_forwarded(k - 1)
    feed_forwarded(Z - 1)

    gate = acc_g[...]
    hidden = (gate / (1.0 + jnp.exp(-gate)) * acc_u[...]).astype(BF16)

    def down(j):
        span = pl.ds(pl.multiple_of(j * W, 128), W)
        pltpu.make_async_copy(wd_hbm.at[0, :, span], wd.at[j], wd_sem.at[j]).wait()
        return jnp.dot(hidden, wd[j], preferred_element_type=F32)

    z_order = sorted(range(Z), key=lambda k: -min(k, Z - k))
    for k in z_order:
        zz = at(k, Z, z)
        for b in range(1, B):
            cc = at(b, B, c)
            part[b - 1, zz] = down(cc * Z + zz).astype(BF16)
            copy = pltpu.make_async_remote_copy(
                src_ref=part.at[b - 1, zz], dst_ref=pr.at[b - 1, zz],
                send_sem=p_send.at[b - 1, zz], recv_sem=p_recv.at[b - 1, zz],
                device_id=(a, cc, z), device_id_type=MESH,
            )
            copy.start()
            sends.append(copy)
    for k in z_order:
        zz = at(k, Z, z)
        value = down(c * Z + zz)
        for b in range(1, B):
            pltpu.make_async_remote_copy(
                src_ref=part.at[b - 1, zz], dst_ref=pr.at[b - 1, zz],
                send_sem=p_send.at[b - 1, zz], recv_sem=p_recv.at[b - 1, zz],
                device_id=(a, at(b, B, c), z), device_id_type=MESH,
            ).wait_recv()
            value = value + pr[b - 1, zz].astype(F32)
        for e in range(E):
            total[zz, e] = value[e * CAP : (e + 1) * CAP, :].astype(BF16)
        for i in range(E):
            aa = at(i, E, a)
            if (k, i) == (0, 0):
                rr[a, z] = total[z, a]
                continue
            copy = pltpu.make_async_remote_copy(
                src_ref=total.at[zz, aa], dst_ref=rr.at[a, z],
                send_sem=r_send.at[zz, aa], recv_sem=r_recv.at[a, z],
                device_id=(aa, c, zz), device_id_type=MESH,
            )
            copy.start()
            sends.append(copy)

    for k in range(Z):
        for i in range(E):
            if (k, i) != (0, 0):
                aa, zz = at(i, E, a), at(k, Z, z)
                pltpu.make_async_remote_copy(
                    src_ref=rr.at[aa, zz], dst_ref=rr.at[aa, zz],
                    send_sem=r_send.at[zz, aa], recv_sem=r_recv.at[aa, zz],
                    device_id=(a, at(1, B, c), z), device_id_type=MESH,
                ).wait_recv()
    outs = []
    for e in range(E):
        value = rr[e, 0].astype(F32)
        for k in range(1, Z):
            value = value + rr[e, k].astype(F32)
        outs.append(value)
    merged = jnp.concatenate(outs, axis=0).astype(BF16)
    merged_ref[0:rows, :] = merged
    merged_ref[rows : 2 * rows, :] = merged
    for copy in sends:
        copy.wait_send()


def shards(E, B, Z, tokens, expert_ids, route_weight, w_gate, w_up, w_down):
    T, W = tokens.shape
    H = w_gate.shape[2]
    N = B * Z
    rows = E * CAP
    top = expert_ids.shape[1]
    dma = pltpu.SemaphoreType.DMA
    vmem = pltpu.VMEM
    merged, wt = pl.pallas_call(
        functools.partial(kernel, E, B, Z),
        out_shape=(
            jax.ShapeDtypeStruct((2 * rows, W), BF16),
            jax.ShapeDtypeStruct((2 * rows, T), BF16),
        ),
        in_specs=[pl.BlockSpec(memory_space=pl.ANY)] * 6,
        out_specs=(pl.BlockSpec(memory_space=vmem), pl.BlockSpec(memory_space=vmem)),
        scratch_shapes=[
            vmem((top, T), jnp.int32),
            vmem((top, T), F32),
            vmem((T, W), BF16),
            vmem((N, W, H), BF16),
            vmem((N, W, H), BF16),
            vmem((N, H, W), BF16),
            vmem((E, CAP, W), BF16),
            vmem((N, E, CAP, W), BF16),
            vmem((rows, H), F32),
            vmem((rows, H), F32),
            vmem((B - 1, Z, rows, W), BF16),
            vmem((B - 1, Z, rows, W), BF16),
            vmem((Z, E, CAP, W), BF16),
            vmem((E, Z, CAP, W), BF16),
            dma((3,)), dma((N,)), dma((N,)), dma((N,)),
            dma((Z, E)), dma((Z, E)),
            dma((B - 1, Z)), dma((B - 1, Z)),
            dma((B - 1, Z)), dma((B - 1, Z)),
            dma((Z, E)), dma((E, Z)),
        ],
        compiler_params=pltpu.CompilerParams(collective_id=0, has_side_effects=True),
    )(expert_ids.T, route_weight.T, tokens, w_gate, w_up, w_down)
    mixed = lax.dot_general(
        wt, merged, (((0,), (0,)), ((), ())), preferred_element_type=F32
    )
    return mixed.astype(BF16)


def solution(mesh):
    in_specs = (
        P("aa", ("ba", "col")),
        P("aa", None),
        P("aa", None),
        P("aa", None, ("ba", "col")),
        P("aa", None, ("ba", "col")),
        P("aa", ("ba", "col"), None),
    )
    out_specs = P("aa", ("ba", "col"))
    body = functools.partial(shards, mesh.shape["aa"], mesh.shape["ba"], mesh.shape["col"])
    return jax.shard_map(body, mesh=mesh, in_specs=in_specs, out_specs=out_specs, check_vma=False)
```

time: 134 us -> 27.6 us (0.21)
  blocking collectives: 47.4 us -> 0 us
  waiting for transfers between devices: 41.1 us -> 0 us
  Pallas kernels: 0 us -> 25.4 us
  local copies, waits for them, and re-layouts: 19.9 us -> 0 us
  between operations: 13.4 us -> 0.01 us
  matrix products: 9.63 us -> 2 us
  other arithmetic: 2.13 us -> 0 us
    unnamed x2 -> x0, waiting for transfers between devices: 41.1 us -> none
    all_gather x1 -> x0, blocking collectives: 26.4 us -> none  [shards(): portion = lax.all_gather(flat_rows, ('ba', 'col'), axis=1, tiled=True)]
    pallas_call x0 -> x1, Pallas kernels: none -> 25.4 us  [shards(): pl.pallas_call(functools.partial(kernel, E, B, Z), out_shape=(jax.ShapeDt...]
    all_to_all x2 -> x0, blocking collectives: 21 us -> none  [the longest x1 11.2 us: shards(): lax.all_to_all(shaped, 'aa', split_axis=0, concat_axis=0, tiled=True)]
    unnamed x10 -> x0, local copies, waits for them, and re-layouts: 19.6 us -> none
    dot_general x5 -> x1, matrix products: 9.63 us -> 2 us  [shards(): lax.dot_general(wt, merged, (((0,), (0,)), ((), ())), preferred_element_t...]
  transfers between devices with their start and end apart: 1 -> 0, of which waited for: 1 -> 0; matrix products, arithmetic and copies ran while one was open for 0% -> 0% of each run, Pallas kernels for 0% -> 0%
where the time goes in v1:
time: 27.6 us; the launch traced here: 27.4 us
  Pallas kernels  25.4 us (92%)
  matrix products  2 us (7%)
    pallas_call x1, Pallas kernels, shards(): pl.pallas_call(functools.partial(kernel, E, B, Z), out_shape=(jax.ShapeDt...  25.4 us
    dot_general x1, matrix products, shards(): lax.dot_general(wt, merged, (((0,), (0,)), ((), ())), preferred_element_t...  2 us

profile of v1, /device:TPU:0, one launch (start us, length us, event | category | flops | bytes accessed | tf_op | source)
XLA Modules:
  0.0 27.4 jit_solution(17376132637297561337)
XLA Ops:
  0.0 25.4 %shard_map.64 = (bf16[64,896]{1,0:T(8,128)(2,1)}, bf16[64,256]{1,0:T(8,128)(2,1)}) custom-call(s32[8,256]{1,0:T(8,128)} %bitcast.4, f32[8,256]{1,0:T(8,128)} %bitcast.5, bf16[256,896]{1,0:T(8,128)(2,1)} %tok_hbm.1, bf16[1,7168,256]{2,1,0:T(8,128)(2,1)} %wg_hbm.1, bf16[1,7168,256]{2,1,0:T(8,128)(2,1)} %wu_hbm.1, bf16[1,256,7168]{2,1,0:T(8,128)(2,1)} %wd_hbm.1), custom_call_target="tpu_custom_call" | custom-call | tf_op jit(solution)/shard_map/pallas_call | solution.py:244
  25.4 2.0 %convolution_convert_fusion = bf16[256,896]{1,0:T(8,128)(2,1)} fusion(bf16[64,256]{1,0:T(8,128)(2,1)} %get-tuple-element.7, bf16[64,896]{1,0:T(8,128)(2,1)} %get-tuple-element.8), kind=kOutput, calls=%fused_computation | convolution fusion | flops 29589504 | bytes 606208 | tf_op jit(solution)/shard_map/dot_general | solution.py:275

commit v2 on v1

--- a/solution.py
+++ b/solution.py
@@ -17,7 +17,7 @@
     E, B, Z,
     ids_hbm, rw_hbm, tok_hbm, wg_hbm, wu_hbm, wd_hbm,
     merged_ref, wt_ref,
-    ids, rw, tok, wg, wu, wd, disp, xr, acc_g, acc_u, part, pr, total, rr,
+    ids, rw, tok, wg, wu, wd, disp, xr, acc_g, acc_u, own, part, pr, total, rr,
     in_sem, wg_sem, wu_sem, wd_sem,
     d_send, d_recv, f_send, f_recv, p_send, p_recv, r_send, r_recv,
 ):
@@ -29,16 +29,22 @@
     W = tok.shape[1]
     rows = E * CAP
 
+    def at(k, n, base):
+        return lax.rem(base + k, n)
+
+    if Z == 4:
+        half = z // 2
+        near = [z, z + 1 - 2 * lax.rem(z, 2), 2 - half, 3 - 3 * half]
+    else:
+        near = [lax.rem(z + k, Z) for k in range(Z)]
+
     def far_first():
         order = []
-        for k in sorted(range(Z), key=lambda k: -min(k, Z - k)):
+        for k in list(range(2, Z))[::-1] + list(range(min(Z, 2)))[::-1]:
             for i in range(E):
                 if (k, i) != (0, 0):
                     order.append((k, i))
         return order
-
-    def at(k, n, base):
-        return lax.rem(base + k, n)
 
     ins = [
         pltpu.make_async_copy(ids_hbm, ids, in_sem.at[0]),
@@ -51,12 +57,12 @@
     barrier = pltpu.get_barrier_semaphore()
     for k, i in far_first():
         pl.semaphore_signal(
-            barrier, inc=1, device_id=(at(i, E, a), c, at(k, Z, z)), device_id_type=MESH
+            barrier, inc=1, device_id=(at(i, E, a), c, near[k]), device_id_type=MESH
         )
     for b in range(1, B):
         pl.semaphore_signal(barrier, inc=1, device_id=(a, at(b, B, c), z), device_id_type=MESH)
 
-    chunks = [(at(b, B, c), at(k, Z, z)) for k in range(Z) for b in range(B)]
+    chunks = [(at(b, B, c), near[k]) for k in range(Z) for b in range(B)]
     w_copies = []
     for cc, zz in chunks:
         j = cc * Z + zz
@@ -105,7 +111,7 @@
 
     sends = []
     for k, i in far_first():
-        aa, zz = at(i, E, a), at(k, Z, z)
+        aa, zz = at(i, E, a), near[k]
         copy = pltpu.make_async_remote_copy(
             src_ref=disp.at[aa], dst_ref=xr.at[mine, a],
             send_sem=d_send.at[zz, aa], recv_sem=d_recv.at[z, a],
@@ -115,9 +121,8 @@
         sends.append(copy)
 
     weight = jnp.concatenate(weights, axis=0)
-    high = weight.astype(BF16)
-    low = (weight - high.astype(F32)).astype(BF16)
-    wt_ref[...] = jnp.concatenate([high, low], axis=0)
+    high = weight.astype(BF16).astype(F32)
+    wt_ref[...] = jnp.concatenate([high, weight - high], axis=0).T.astype(BF16)
 
     acc_g[...] = jnp.zeros_like(acc_g)
     acc_u[...] = jnp.zeros_like(acc_u)
@@ -131,7 +136,7 @@
         acc_u[...] += jnp.dot(x, wu[j], preferred_element_type=F32)
 
     def feed_forwarded(k):
-        zz = at(k, Z, z)
+        zz = near[k]
         for b in range(1, B):
             j = at(B - b, B, c) * Z + zz
             pltpu.make_async_remote_copy(
@@ -142,7 +147,7 @@
             feed(j)
 
     for k in range(Z):
-        zz = at(k, Z, z)
+        zz = near[k]
         j = c * Z + zz
         for i in range(E):
             if (k, i) != (0, 0):
@@ -173,9 +178,10 @@
         pltpu.make_async_copy(wd_hbm.at[0, :, span], wd.at[j], wd_sem.at[j]).wait()
         return jnp.dot(hidden, wd[j], preferred_element_type=F32)
 
-    z_order = sorted(range(Z), key=lambda k: -min(k, Z - k))
-    for k in z_order:
-        zz = at(k, Z, z)
+    z_order = list(range(2, Z))[::-1] + list(range(min(Z, 2)))[::-1]
+
+    def exchange(k):
+        zz = near[k]
         for b in range(1, B):
             cc = at(b, B, c)
             part[b - 1, zz] = down(cc * Z + zz).astype(BF16)
@@ -186,9 +192,9 @@
             )
             copy.start()
             sends.append(copy)
-    for k in z_order:
-        zz = at(k, Z, z)
-        value = down(c * Z + zz)
+
+    def give_back(k, value):
+        zz = near[k]
         for b in range(1, B):
             pltpu.make_async_remote_copy(
                 src_ref=part.at[b - 1, zz], dst_ref=pr.at[b - 1, zz],
@@ -211,10 +217,18 @@
             copy.start()
             sends.append(copy)
 
+    for k in z_order[:2]:
+        exchange(k)
+    for n, k in enumerate(z_order):
+        own[...] = down(c * Z + near[k])
+        if n + 2 < Z:
+            exchange(z_order[n + 2])
+        give_back(k, own[...])
+
     for k in range(Z):
         for i in range(E):
             if (k, i) != (0, 0):
-                aa, zz = at(i, E, a), at(k, Z, z)
+                aa, zz = at(i, E, a), near[k]
                 pltpu.make_async_remote_copy(
                     src_ref=rr.at[aa, zz], dst_ref=rr.at[aa, zz],
                     send_sem=r_send.at[zz, aa], recv_sem=r_recv.at[aa, zz],
@@ -241,13 +255,14 @@
     top = expert_ids.shape[1]
     dma = pltpu.SemaphoreType.DMA
     vmem = pltpu.VMEM
+    limit = 2 * (3 * N * W * H + T * W + 8 * N * rows * W) + 4 * 1024 * 1024
     merged, wt = pl.pallas_call(
         functools.partial(kernel, E, B, Z),
         out_shape=(
             jax.ShapeDtypeStruct((2 * rows, W), BF16),
-            jax.ShapeDtypeStruct((2 * rows, T), BF16),
+            jax.ShapeDtypeStruct((T, 2 * rows), BF16),
         ),
-        in_specs=[pl.BlockSpec(memory_space=pl.ANY)] * 6,
+        in_specs=[pl.BlockSpec(memory_space=pltpu.HBM)] * 6,
         out_specs=(pl.BlockSpec(memory_space=vmem), pl.BlockSpec(memory_space=vmem)),
         scratch_shapes=[
             vmem((top, T), jnp.int32),
@@ -260,6 +275,7 @@
             vmem((N, E, CAP, W), BF16),
             vmem((rows, H), F32),
             vmem((rows, H), F32),
+            vmem((rows, W), F32),
             vmem((B - 1, Z, rows, W), BF16),
             vmem((B - 1, Z, rows, W), BF16),
             vmem((Z, E, CAP, W), BF16),
@@ -270,12 +286,12 @@
             dma((B - 1, Z)), dma((B - 1, Z)),
             dma((Z, E)), dma((E, Z)),
         ],
-        compiler_params=pltpu.CompilerParams(collective_id=0, has_side_effects=True),
-    )(expert_ids.T, route_weight.T, tokens, w_gate, w_up, w_down)
-    mixed = lax.dot_general(
-        wt, merged, (((0,), (0,)), ((), ())), preferred_element_type=F32
-    )
-    return mixed.astype(BF16)
+        compiler_params=pltpu.CompilerParams(collective_id=0, has_side_effects=True, vmem_limit_bytes=limit),
+    )(*(
+        pltpu.with_memory_space_constraint(x, pltpu.HBM)
+        for x in (expert_ids.T, route_weight.T, tokens, w_gate, w_up, w_down)
+    ))
+    return jnp.dot(wt, merged, preferred_element_type=F32).astype(BF16)
 
 
 def solution(mesh):

time: 27.6 us -> 25.4 us (0.920)
  Pallas kernels: 25.4 us -> 24.1 us
  matrix products: 2 us -> 1.02 us
    pallas_call x1, Pallas kernels: 25.4 us -> 24.1 us  [shards(): pl.pallas_call(functools.partial(kernel, E, B, Z), out_shape=(jax.ShapeDt...]
    dot_general x1, matrix products: 2 us -> 1.02 us  [shards(): return jnp.dot(wt, merged, preferred_element_type=F32).astype(BF16)]
where the time goes in v2:
time: 25.4 us; the launch traced here: 25.2 us
  Pallas kernels  24.1 us (95%)
  matrix products  1.02 us (4%)
    pallas_call x1, Pallas kernels, shards(): pl.pallas_call(functools.partial(kernel, E, B, Z), out_shape=(jax.ShapeDt...  24.1 us
    dot_general x1, matrix products, shards(): return jnp.dot(wt, merged, preferred_element_type=F32).astype(BF16)  1.02 us

profile of v2, /device:TPU:0, one launch (start us, length us, event | category | flops | bytes accessed | tf_op | source)
XLA Modules:
  0.0 25.2 jit_solution(7746907638706214434)
XLA Ops:
  0.0 24.1 %shard_map.64 = (bf16[64,896]{1,0:T(8,128)(2,1)S(1)}, bf16[256,64]{1,0:T(8,128)(2,1)S(1)}) custom-call(s32[8,256]{1,0:T(8,128)} %bitcast.4, f32[8,256]{1,0:T(8,128)} %bitcast.5, bf16[256,896]{1,0:T(8,128)(2,1)} %tok_hbm.1, bf16[1,7168,256]{2,1,0:T(8,128)(2,1)} %wg_hbm.1, bf16[1,7168,256]{2,1,0:T(8,128)(2,1)} %wu_hbm.1, bf16[1,256,7168]{2,1,0:T(8,128)(2,1)} %wd_hbm.1), custom_call_target="tpu_custom_call" | custom-call | tf_op jit(solution)/shard_map/pallas_call | solution.py:259
  24.2 1.0 %convolution_convert_fusion = bf16[256,896]{1,0:T(8,128)(2,1)} fusion(bf16[256,64]{1,0:T(8,128)(2,1)S(1)} %get-tuple-element.7, bf16[64,896]{1,0:T(8,128)(2,1)S(1)} %get-tuple-element.8), kind=kOutput, calls=%fused_computation | convolution fusion | flops 29589504 | bytes 606208 | tf_op jit(solution)/shard_map/dot_general | solution.py:294

commit v3 on v2

--- a/solution.py
+++ b/solution.py
@@ -38,10 +38,10 @@
     else:
         near = [lax.rem(z + k, Z) for k in range(Z)]
 
-    def far_first():
+    def peers():
         order = []
-        for k in list(range(2, Z))[::-1] + list(range(min(Z, 2)))[::-1]:
-            for i in range(E):
+        for k in list(range(Z)):
+            for i in range(E)[::-1]:
                 if (k, i) != (0, 0):
                     order.append((k, i))
         return order
@@ -55,7 +55,7 @@
         copy.start()
 
     barrier = pltpu.get_barrier_semaphore()
-    for k, i in far_first():
+    for k, i in peers():
         pl.semaphore_signal(
             barrier, inc=1, device_id=(at(i, E, a), c, near[k]), device_id_type=MESH
         )
@@ -110,7 +110,7 @@
     pl.semaphore_wait(barrier, E * Z - 1 + B - 1)
 
     sends = []
-    for k, i in far_first():
+    for k, i in peers():
         aa, zz = at(i, E, a), near[k]
         copy = pltpu.make_async_remote_copy(
             src_ref=disp.at[aa], dst_ref=xr.at[mine, a],
@@ -204,7 +204,7 @@
             value = value + pr[b - 1, zz].astype(F32)
         for e in range(E):
             total[zz, e] = value[e * CAP : (e + 1) * CAP, :].astype(BF16)
-        for i in range(E):
+        for i in range(E)[::-1]:
             aa = at(i, E, a)
             if (k, i) == (0, 0):
                 rr[a, z] = total[z, a]
@@ -217,12 +217,12 @@
             copy.start()
             sends.append(copy)
 
-    for k in z_order[:2]:
+    for k in z_order[:1]:
         exchange(k)
     for n, k in enumerate(z_order):
         own[...] = down(c * Z + near[k])
-        if n + 2 < Z:
-            exchange(z_order[n + 2])
+        if n + 1 < Z:
+            exchange(z_order[n + 1])
         give_back(k, own[...])
 
     for k in range(Z):

time: 25.4 us -> 24 us (0.945)
  Pallas kernels: 24.1 us -> 22.7 us
    pallas_call x1, Pallas kernels: 24.1 us -> 22.7 us  [shards(): pl.pallas_call(functools.partial(kernel, E, B, Z), out_shape=(jax.ShapeDt...]
where the time goes in v3:
time: 24 us; the launch traced here: 23.8 us
  Pallas kernels  22.7 us (95%)
  matrix products  1.03 us (4%)
    pallas_call x1, Pallas kernels, shards(): pl.pallas_call(functools.partial(kernel, E, B, Z), out_shape=(jax.ShapeDt...  22.7 us
    dot_general x1, matrix products, shards(): return jnp.dot(wt, merged, preferred_element_type=F32).astype(BF16)  1.03 us

profile of v3, /device:TPU:0, one launch (start us, length us, event | category | flops | bytes accessed | tf_op | source)
XLA Modules:
  0.0 23.8 jit_solution(6329472552017506144)
XLA Ops:
  0.0 22.7 %shard_map.64 = (bf16[64,896]{1,0:T(8,128)(2,1)S(1)}, bf16[256,64]{1,0:T(8,128)(2,1)S(1)}) custom-call(s32[8,256]{1,0:T(8,128)} %bitcast.4, f32[8,256]{1,0:T(8,128)} %bitcast.5, bf16[256,896]{1,0:T(8,128)(2,1)} %tok_hbm.1, bf16[1,7168,256]{2,1,0:T(8,128)(2,1)} %wg_hbm.1, bf16[1,7168,256]{2,1,0:T(8,128)(2,1)} %wu_hbm.1, bf16[1,256,7168]{2,1,0:T(8,128)(2,1)} %wd_hbm.1), custom_call_target="tpu_custom_call" | custom-call | tf_op jit(solution)/shard_map/pallas_call | solution.py:259
  22.7 1.0 %convolution_convert_fusion = bf16[256,896]{1,0:T(8,128)(2,1)} fusion(bf16[256,64]{1,0:T(8,128)(2,1)S(1)} %get-tuple-element.7, bf16[64,896]{1,0:T(8,128)(2,1)S(1)} %get-tuple-element.8), kind=kOutput, calls=%fused_computation | convolution fusion | flops 29589504 | bytes 606208 | tf_op jit(solution)/shard_map/dot_general | solution.py:294
